TPU v7x, 32 devices: a whole 2x2x4 slice. The times are simulated.
32 devices in a mesh: dp: 8 (over z, x), tp: 4 (over y, core).
Axes of the slice: x: 2, y: 2, z: 4, core: 2. Of those that a mesh axis runs over, the one named last changes fastest.
Arguments:
- queries: bfloat16 [512, 73728], P('dp', 'tp'), may hold values from -32 to 32
- prefix_cache: bfloat16 [8, 576, 1024], P('dp', None, 'tp'), may hold values from -12 to 12
- suffix_cache: bfloat16 [512, 576, 128], P('dp'), may hold values from -48 to 48
- w_uv: bfloat16 [128, 512, 128], P('tp'), may hold values from -1 to 1
- fork_prompt: int32 [512, 1], P('dp'), may hold values from 0 to 7; in each aligned block of 64 rows (0 to 63, 64 to 127, ...) at most 16 rows name the same one
- prompt_slot: int32 [8], replicated, may hold values from 0 to 7, each once
- suffix_len: int32 [512], P('dp'), may hold values from 32 to 128
Outputs:
- attended: bfloat16 [512, 16384], P('dp', 'tp')
Inputs may be any that keep to these rules, and one draw needn't show every extreme that they name: `fork_prompt`: among the 64 forks of one index of dp no prompt is named more than 16 times. `prompt_slot`: each slot holds exactly one prompt.
All inputs are finite; a program needn't handle non-finite values.
Results may differ from a plain program's by a relative error of at most 0.033.
Values may be sent and summed in bfloat16 or wider, within the bound.
A program may use at most 128 MiB of HBM per device.

v0:
```python
import functools

import jax
import jax.numpy as jnp
from jax import lax
from jax.experimental import pallas as pl
from jax.experimental.pallas import tpu as pltpu
from jax.sharding import PartitionSpec as P

R = 512
P_SIZE = 64
V = 128


score_scale = 192.0 ** (-0.5)
log2e = 1.4426950408889634
OUTER = (((1,), (1,)), ((), ()))


def project(latent, w_uv):
    return jnp.einsum("nhr,hrv->nhv", latent, w_uv, preferred_element_type=jnp.float32).astype(
        jnp.bfloat16
    )


def exchange_plan(queries, prefix_cache, suffix_cache, w_uv, fork_prompt, prompt_slot, suffix_len):
    owners_count = lax.axis_size("dp")
    forks_here = queries.shape[0]
    heads_here = w_uv.shape[0]
    key_width = R + P_SIZE
    capacity = max(2, 2 * forks_here // owners_count)
    slots_all = owners_count * capacity
    prompt_ids = jnp.arange(prompt_slot.shape[0], dtype=jnp.int32)
    chosen = fork_prompt[:, 0][:, None] == prompt_ids[None, :]
    owner_slot = jnp.sum(jnp.where(chosen, prompt_slot[None, :], 0), axis=1)
    fork_order = jnp.arange(forks_here, dtype=jnp.int32)
    before = (owner_slot[:, None] == owner_slot[None, :]) & (
        fork_order[None, :] < fork_order[:, None]
    )
    slot_rank = jnp.sum(before.astype(jnp.int32), axis=1)
    target = owner_slot * capacity + slot_rank
    placing = target[None, :] == jnp.arange(slots_all, dtype=jnp.int32)[:, None]
    outbound = jnp.dot(
        placing.astype(jnp.bfloat16), queries, preferred_element_type=jnp.float32
    ).astype(jnp.bfloat16)
    outbound = outbound.reshape(owners_count, capacity, heads_here * key_width)
    gathered = lax.all_gather(prefix_cache, "tp", axis=2, tiled=True)[0]
    received = lax.all_to_all(outbound, "dp", split_axis=0, concat_axis=0, tiled=True)
    sources = received.shape[0]
    items = received.shape[1]
    lead_rows = sources * items
    query_rows = received.reshape(lead_rows * heads_here, key_width)
    scores = jnp.dot(query_rows, gathered, preferred_element_type=jnp.float32) * score_scale
    peak_score = jnp.max(scores, axis=1, keepdims=True)
    weights = jnp.exp(scores - peak_score)
    mass_sum = jnp.sum(weights, axis=1)
    summed = lax.dot_general(
        weights.astype(jnp.bfloat16),
        gathered[:R],
        (((1,), (1,)), ((), ())),
        preferred_element_type=jnp.float32,
    )
    latent = (summed / mass_sum[:, None]).astype(jnp.bfloat16)
    log_mass = (peak_score[:, 0] + jnp.log(mass_sum)).reshape(sources, items, heads_here)
    result = project(latent.reshape(lead_rows, heads_here, R), w_uv)
    result = result.reshape(sources, items, heads_here * V)
    answer, answer_mass = (
        lax.all_to_all(result, "dp", split_axis=0, concat_axis=0, tiled=True),
        lax.all_to_all(
            log_mass.astype(jnp.bfloat16), "dp", split_axis=0, concat_axis=0, tiled=True
        ).astype(log_mass.dtype),
    )
    picking = placing.astype(jnp.bfloat16)
    flat_answer = answer.reshape(slots_all, answer.shape[2])
    returned = lax.dot_general(
        picking, flat_answer, (((0,), (0,)), ((), ())), preferred_element_type=jnp.float32
    ).astype(jnp.bfloat16)
    mass_prefix = lax.dot_general(
        placing.astype(jnp.float32),
        answer_mass.reshape(slots_all, heads_here),
        (((0,), (0,)), ((), ())),
        precision=lax.Precision.HIGHEST,
    )
    value_prefix = returned.reshape(forks_here, heads_here, V)
    query_heads = queries.reshape(forks_here, heads_here, key_width)
    suffix_scores = (
        jnp.einsum("fhe,fes->fhs", query_heads, suffix_cache, preferred_element_type=jnp.float32)
        * score_scale
    )
    positions = jnp.arange(suffix_cache.shape[2], dtype=jnp.int32)
    live_mask = (positions[None, :] < suffix_len[:, None])[:, None, :]
    suffix_scores = jnp.where(live_mask, suffix_scores, -jnp.inf)
    suffix_peak = jnp.max(suffix_scores, axis=2, keepdims=True)
    suffix_weights = jnp.where(live_mask, jnp.exp(suffix_scores - suffix_peak), 0.0)
    suffix_sum = jnp.sum(suffix_weights, axis=2)
    suffix_summed = jnp.einsum(
        "fhs,frs->fhr",
        suffix_weights.astype(jnp.bfloat16),
        suffix_cache[:, :R, :],
        preferred_element_type=jnp.float32,
    )
    latent_suffix = (suffix_summed / suffix_sum[..., None]).astype(jnp.bfloat16)
    mass_suffix = suffix_peak[..., 0] + jnp.log(suffix_sum)
    value_suffix = project(latent_suffix, w_uv)
    top_mass = jnp.maximum(mass_prefix, mass_suffix)
    share_prefix = jnp.exp(mass_prefix - top_mass)[..., None]
    share_suffix = jnp.exp(mass_suffix - top_mass)[..., None]
    combined = (
        share_prefix * value_prefix.astype(jnp.float32)
        + share_suffix * value_suffix.astype(jnp.float32)
    ) / (share_prefix + share_suffix)
    return combined.astype(jnp.bfloat16).reshape(forks_here, heads_here * V)


MESH = pl.DeviceIdType.MESH


def suffix_fork(i, lens_ref, q_ref, cache_ref, latent_ref, mass_ref):
    positions = lax.broadcasted_iota(jnp.int32, (1, cache_ref.shape[2]), 1)
    live = positions < lens_ref[i]
    scores = jnp.dot(q_ref[i], cache_ref[i], preferred_element_type=jnp.float32)
    scores = jnp.where(live, scores * score_scale, -jnp.inf)
    peak = jnp.max(scores, axis=1, keepdims=True)
    weights = jnp.exp(scores - peak)
    mass = jnp.sum(weights, axis=1, keepdims=True)
    summed = lax.dot_general(
        weights.astype(jnp.bfloat16),
        cache_ref[i, :R, :],
        OUTER,
        preferred_element_type=jnp.float32,
    )
    latent_ref[i] = (summed / mass).astype(jnp.bfloat16)
    mass_ref[i] = jnp.broadcast_to(peak + jnp.log(mass), mass_ref.shape[1:])


def gather_kernel(
    planes,
    steps,
    lens_ref,
    own_ref,
    q_ref,
    suffix_ref,
    out_ref,
    latent_ref,
    mass_ref,
    held,
    load_sem,
    own_sem,
    z_send,
    z_recv,
    x_send,
    x_recv,
    y_send,
    y_recv,
    dx_send,
    dx_recv,
    dy_send,
    dy_recv,
    pair_send,
    pair_recv,
):
    dp, tp = lax.axis_index("dp"), lax.axis_index("tp")
    z, x = dp // 2, dp % 2
    y, c = tp // 2, tp % 2
    forks = q_ref.shape[0]
    block = forks // steps
    half = own_ref.shape[1] // 2
    at_x = (z * 2 + (1 - x), tp)
    at_y = (dp, (1 - y) * 2 + c)
    at_pair = (dp, y * 2 + (1 - c))
    at_up = (jnp.minimum(z + 1, planes - 1) * 2 + x, tp)
    at_down = (jnp.maximum(z - 1, 0) * 2 + x, tp)
    has_up, has_down = z + 1 < planes, z > 0

    def place(zz, xx, yy):
        return out_ref.at[zz * 2 + xx, yy * 2 + c]

    def top(ref):
        return ref.at[pl.ds(0, half)]

    def bottom(ref):
        return ref.at[pl.ds(half, half)]

    def copy(src, dst, send, recv, device):
        return pltpu.make_async_remote_copy(
            src_ref=src,
            dst_ref=dst,
            send_sem=send,
            recv_sem=recv,
            device_id=device,
            device_id_type=MESH,
        )

    def z_copy(zz, device, src=None):
        to = place(zz, x, y)
        return copy(to if src is None else src, to, z_send.at[zz], z_recv.at[zz], device)

    def own_up(device, src):
        to = place(z, x, y)
        return copy(src, to, z_send.at[planes], z_recv.at[z], device)

    def x_copy(zz, src=None):
        to = place(zz, x, y)
        return copy(to if src is None else src, to, x_send.at[zz], x_recv.at[zz], at_x)

    def y_copy(zz, src=None):
        to = place(zz, x, y)
        return copy(to if src is None else src, to, y_send.at[zz], y_recv.at[zz], at_y)

    def dy_copy(zz):
        part = top(place(zz, 1 - x, y))
        return copy(part, part, dy_send.at[zz], dy_recv.at[zz], at_y)

    def dx_copy(zz):
        part = bottom(place(zz, x, 1 - y))
        return copy(part, part, dx_send.at[zz], dx_recv.at[zz], at_x)

    def pair_copy(zz, xx, yy, src=None):
        to = place(zz, xx, yy)
        k = (zz * 2 + xx) * 2 + yy
        src = to if src is None else src
        return copy(src, to, pair_send.at[k], pair_recv.at[k], at_pair)

    def load(s):
        part = pl.ds(s * block, block)
        return pltpu.make_async_copy(suffix_ref.at[part], held.at[part], load_sem.at[s])

    for s in range(steps):
        load(s).start()

    barrier = pltpu.get_barrier_semaphore()
    for device in (at_x, at_y, at_pair):
        pl.semaphore_signal(barrier, inc=1, device_id=device, device_id_type=MESH)

    @pl.when(has_up)
    def _():
        pl.semaphore_signal(barrier, inc=1, device_id=at_up, device_id_type=MESH)

    @pl.when(has_down)
    def _():
        pl.semaphore_signal(barrier, inc=1, device_id=at_down, device_id_type=MESH)

    pl.semaphore_wait(barrier, 3 + has_up.astype(jnp.int32) + has_down.astype(jnp.int32))

    mine = own_ref.at[0]

    @pl.when(has_up)
    def _():
        z_copy(z, at_up, mine).start()

    @pl.when(has_down)
    def _():
        own_up(at_down, mine).start()

    x_copy(z, mine).start()
    y_copy(z, mine).start()
    pair_copy(z, x, y, mine).start()
    local = pltpu.make_async_copy(mine, place(z, x, y), own_sem)
    local.start()

    def compute(low, high):
        def step(s, carry):
            load(s).wait()
            for i in range(block):
                suffix_fork(s * block + i, lens_ref, q_ref, held, latent_ref, mass_ref)
            return carry

        lax.fori_loop(low, high, step, 0)

    def arrived(d):
        for sign in (-1, 1):
            zz = z + sign * d
            onward = has_up if sign < 0 else has_down
            device = at_up if sign < 0 else at_down

            @pl.when((zz >= 0) & (zz < planes))
            def _():
                z_copy(zz, device).wait_recv()

                @pl.when(onward)
                def _():
                    z_copy(zz, device).start()

                x_copy(zz).start()
                y_copy(zz).start()
                pair_copy(zz, x, y).start()

    def each(d, act):
        if d == 0:
            act(z)
            return
        for sign in (-1, 1):
            zz = z + sign * d
            pl.when((zz >= 0) & (zz < planes))(functools.partial(act, zz))

    def across(zz):
        x_copy(zz).wait_recv()
        dy_copy(zz).start()
        pair_copy(zz, 1 - x, y).start()
        y_copy(zz).wait_recv()
        dx_copy(zz).start()
        pair_copy(zz, x, 1 - y).start()

    def diagonal(zz):
        dy_copy(zz).wait_recv()
        dx_copy(zz).wait_recv()
        pair_copy(zz, 1 - x, 1 - y).start()

    marks = [min(steps, 3 * r * steps // 8) for r in range(planes)]
    marks[-1] = steps
    for r in range(planes):
        if r > 0:
            arrived(r)
            each(r - 1, across)
        if r < planes - 1:
            compute(marks[r], marks[r + 1])
    for r in range(planes - 1):
        each(r, diagonal)
    each(planes - 1, across)
    each(planes - 1, diagonal)

    local.wait()

    @pl.when(has_down)
    def _():
        own_up(at_down, mine).wait_send()

    for zz in range(planes):
        sent = ((zz <= z) & has_up) | ((zz > z) & has_down)

        @pl.when(sent)
        def _():
            z_copy(zz, at_up).wait_send()

        x_copy(zz).wait_send()
        y_copy(zz).wait_send()
        dx_copy(zz).wait_send()
        dy_copy(zz).wait_send()
        for xx in range(2):
            for yy in range(2):
                pair_copy(zz, xx, yy).wait()


def gather_and_suffix(prefix_cache, query_heads, suffix_cache, suffix_len, steps=8):
    forks, heads, width = query_heads.shape
    keys = suffix_cache.shape[2]
    slots, parts = lax.axis_size("dp"), lax.axis_size("tp")
    planes = slots // 2
    dma = pltpu.SemaphoreType.DMA
    vmem = pl.BlockSpec(memory_space=pltpu.VMEM)
    hbm = pl.BlockSpec(memory_space=pl.ANY)
    return pl.pallas_call(
        functools.partial(gather_kernel, planes, steps),
        in_specs=[pl.BlockSpec(memory_space=pltpu.SMEM), hbm, vmem, hbm],
        out_specs=[hbm, vmem, vmem],
        out_shape=[
            jax.ShapeDtypeStruct((slots, parts, *prefix_cache.shape[1:]), jnp.bfloat16),
            jax.ShapeDtypeStruct((forks, heads, R), jnp.bfloat16),
            jax.ShapeDtypeStruct((forks, heads, 128), jnp.float32),
        ],
        scratch_shapes=[
            pltpu.VMEM(suffix_cache.shape, jnp.bfloat16),
            dma((steps,)),
            dma,
            dma((planes + 1,)),
            *[dma((planes,)) for _ in range(9)],
            dma((slots * 2,)),
            dma((slots * 2,)),
        ],
        compiler_params=pltpu.CompilerParams(
            collective_id=0, has_side_effects=True, vmem_limit_bytes=40 * 1024 * 1024
        ),
        name="gather",
    )(suffix_len, prefix_cache, query_heads, suffix_cache)


def prefix_kernel(
    group, starts_ref, order_ref, q_ref, cache_ref, latent_ref, mass_ref, out_ref
):
    slot = pl.program_id(0)
    heads = q_ref.shape[1]
    first = starts_ref[slot]
    last = starts_ref[slot + 1] - 1
    parts = cache_ref.shape[1]

    def one_group(g, carry):
        ids = [order_ref[jnp.minimum(first + g * group + i, last)] for i in range(group)]
        rows = jnp.concatenate([q_ref[fork] for fork in ids], axis=0)
        scores = [
            jnp.dot(rows, cache_ref[0, k], preferred_element_type=jnp.float32)
            for k in range(parts)
        ]
        peak = functools.reduce(
            jnp.maximum, [jnp.max(piece, axis=1, keepdims=True) for piece in scores]
        )
        mass = 0.0
        summed = 0.0
        for k in range(parts):
            weights = jnp.exp2((scores[k] - peak) * (score_scale * log2e))
            mass = mass + jnp.sum(weights, axis=1, keepdims=True)
            summed = summed + lax.dot_general(
                weights.astype(jnp.bfloat16),
                cache_ref[0, k, :R, :],
                OUTER,
                preferred_element_type=jnp.float32,
            )
        peak = peak * score_scale
        for i, fork in enumerate(ids):
            own = slice(i * heads, (i + 1) * heads)
            other = mass_ref[fork][:, :1]
            top = jnp.maximum(peak[own], other)
            ours = jnp.exp(peak[own] - top)
            theirs = jnp.exp(other - top)
            share = 1.0 / (ours * mass[own] + theirs)
            out_ref[fork] = (
                summed[own] * (ours * share)
                + latent_ref[fork].astype(jnp.float32) * (theirs * share)
            ).astype(jnp.bfloat16)
        return carry

    lax.fori_loop(0, (last - first + group) // group, one_group, 0)


def prefix_attention(starts, order, query_heads, caches, latent_suffix, mass_suffix, group=8):
    forks, heads, width = query_heads.shape
    slots, parts, _, keys = caches.shape
    whole = lambda s, a, b: (0, 0, 0)
    return pl.pallas_call(
        functools.partial(prefix_kernel, group),
        grid_spec=pltpu.PrefetchScalarGridSpec(
            num_scalar_prefetch=2,
            grid=(slots,),
            in_specs=[
                pl.BlockSpec((forks, heads, width), whole),
                pl.BlockSpec((1, parts, width, keys), lambda s, a, b: (s, 0, 0, 0)),
                pl.BlockSpec((forks, heads, R), whole),
                pl.BlockSpec((forks, heads, 128), whole),
            ],
            out_specs=pl.BlockSpec((forks, heads, R), whole),
        ),
        out_shape=jax.ShapeDtypeStruct((forks, heads, R), jnp.bfloat16),
        cost_estimate=pl.CostEstimate(
            flops=2 * forks * heads * parts * keys * (width + R),
            bytes_accessed=2 * caches.size + 2 * query_heads.size,
            transcendentals=forks * heads * parts * keys,
        ),
        compiler_params=pltpu.CompilerParams(vmem_limit_bytes=48 * 1024 * 1024),
        name="prefix",
    )(starts, order, query_heads, caches, latent_suffix, mass_suffix)


def fork_order(fork_prompt, prompt_slot):
    forks = fork_prompt.shape[0]
    prompt_ids = jnp.arange(prompt_slot.shape[0], dtype=jnp.int32)
    chosen = fork_prompt[:, 0][:, None] == prompt_ids[None, :]
    owner_slot = jnp.sum(jnp.where(chosen, prompt_slot[None, :], 0), axis=1)
    ids = jnp.arange(forks, dtype=jnp.int32)
    key = owner_slot * forks + ids
    place = jnp.sum((key[None, :] < key[:, None]).astype(jnp.int32), axis=1)
    order = jnp.sum(jnp.where(place[None, :] == ids[:, None], ids[None, :], 0), axis=1)
    edges = jnp.arange(prompt_slot.shape[0] + 1, dtype=jnp.int32)
    starts = jnp.sum((owner_slot[None, :] < edges[:, None]).astype(jnp.int32), axis=1)
    return starts, order


def gather_plan(queries, prefix_cache, suffix_cache, w_uv, fork_prompt, prompt_slot, suffix_len):
    forks_here = queries.shape[0]
    heads_here = w_uv.shape[0]
    starts, order = fork_order(fork_prompt, prompt_slot)
    query_heads = queries.reshape(forks_here, heads_here, R + P_SIZE)
    caches, latent_suffix, mass_suffix = gather_and_suffix(
        prefix_cache, query_heads, suffix_cache, suffix_len
    )
    latent = prefix_attention(starts, order, query_heads, caches, latent_suffix, mass_suffix)
    return project(latent, w_uv).reshape(forks_here, heads_here * V)


def shards(queries, prefix_cache, *others):
    owners_count = lax.axis_size("dp")
    forks_here = queries.shape[0]
    capacity = max(2, 2 * forks_here // owners_count)
    sent = owners_count * capacity * queries.shape[1]
    gathered = owners_count * lax.axis_size("tp") * prefix_cache.size
    square = lax.axis_size("tp") == 4 and owners_count % 2 == 0
    plan = gather_plan if square and gathered <= 4 * sent else exchange_plan
    return plan(queries, prefix_cache, *others)


def solution(mesh):
    placed = (
        P("dp", "tp"),
        P("dp", None, "tp"),
        P("dp", None, None),
        P("tp", None, None),
        P("dp", None),
        P(),
        P("dp"),
    )
    return jax.shard_map(
        shards, mesh=mesh, in_specs=placed, out_specs=P("dp", "tp"), check_vma=False
    )
```

profile of v0, /device:TPU:0, one launch (start us, length us, event | category | flops | bytes accessed | tf_op | source)
XLA Modules:
  0.0 74.8 jit_solution(1294510462555938627)
XLA Ops:
  0.0 0.0 copy-start.2
  0.0 0.0 copy-start.1
  0.0 0.8 %select_reduce_fusion.1 = s32[64]{0:T(128)S(1)} fusion(s32[8]{0:T(128)} %param.12, s32[64]{0:T(128)} %bitcast.8), kind=kLoop, calls=%fused_computation.10 | loop fusion | flops 1472 | bytes 544 | tf_op jit(solution)/shard_map/reduce_sum | solution.py:456
  0.8 0.1 convert_reduce_fusion.1.starts_ref
  0.9 0.2 convert_reduce_fusion
  1.1 0.1 select_reduce_fusion.order_ref
  1.2 4.5 %reshape.23.q_ref = bf16[64,32,576]{2,1,0:T(8,128)(2,1)S(1)} reshape(bf16[64,18432]{1,0:T(8,128)(2,1)} %param.7) | data formatting | bytes 4718592 | tf_op jit(solution)/shard_map/reshape | solution.py:470
  5.7 0.0 copy-done.2
  5.7 0.0 copy-done.1
  5.8 0.0 copy-start
  5.8 49.4 %gather.1 = (bf16[8,4,576,256]{3,2,1,0:T(8,128)(2,1)}, bf16[64,32,512]{2,1,0:T(8,128)(2,1)S(1)}, f32[64,32,128]{2,1,0:T(8,128)S(1)}) custom-call(s32[64]{0:T(128)S(1)} %copy-done.2, bf16[1,576,256]{2,1,0:T(8,128)(2,1)S(1)} %copy-done.1, bf16[64,32,576]{2,1,0:T(8,128)(2,1)S(1)} %reshape.23.q_ref, bf16[64,576,128]{2,1,0:T(8,128)(2,1)} %suffix_ref.1), custom_call_target="tpu_custom_call" | custom-call | tf_op jit(solution)/shard_map/gather/pallas_call | solution.py:352
  55.2 0.0 copy-done
  55.2 0.0 copy-start.3
  55.2 16.1 %prefix.1 = bf16[64,32,512]{2,1,0:T(8,128)(2,1)S(1)} custom-call(s32[9]{0:T(128)S(1)} %convert_reduce_fusion.1.starts_ref, s32[64]{0:T(128)S(1)} %select_reduce_fusion.order_ref, bf16[64,32,576]{2,1,0:T(8,128)(2,1)} %copy-done, bf16[8,4,576,256]{3,2,1,0:T(8,128)(2,1)} %get-tuple-element.8.cache_ref, bf16[64,32,512]{2,1,0:T(8,128)(2,1)S(1)} %get-tuple-element.9.latent_ref, ...), custom_call_target="tpu_custom_call" | custom-call | flops 4563402752 | bytes 11796480 | tf_op jit(solution)/shard_map/prefix/pallas_call | solution.py:428
  71.3 0.0 copy-done.3
  71.4 2.5 %fusion.5 = bf16[32,8,8,128]{3,2,1,0:T(8,128)(2,1)S(1)} fusion(bf16[32,512,128]{2,1,0:T(8,128)(2,1)S(1)} %copy-done.3, bf16[64,32,512]{2,1,0:T(8,128)(2,1)S(1)} %prefix.1), kind=kOutput, calls=%fused_computation.3 | convolution fusion | flops 268697600 | bytes 6815744 | tf_op jit(solution)/shard_map/nhr,hrv->nhv/dot_general | solution.py:21
  73.9 0.9 %copy.21 = bf16[32,8,8,128]{3,2,0,1:T(8,128)(2,1)} copy(bf16[32,8,8,128]{3,2,1,0:T(8,128)(2,1)S(1)} %fusion.5) | data formatting | bytes 1048576 | tf_op jit(solution)/shard_map/reshape | solution.py:475
  (1 shorter events, 0.0 us)
Async XLA Ops:
  0.0 5.7 %copy-start.2 = (s32[64]{0:T(128)S(1)}, s32[64]{0:T(128)}, u32[]{:S(2)}) copy-start(s32[64]{0:T(128)} %lens_ref.1) | copy-start | bytes 772
  0.0 5.7 %copy-start.1 = (bf16[1,576,256]{2,1,0:T(8,128)(2,1)S(1)}, bf16[1,576,256]{2,1,0:T(8,128)(2,1)}, u32[]{:S(2)}) copy-start(bf16[1,576,256]{2,1,0:T(8,128)(2,1)} %own_ref.1) | copy-start | bytes 884740
  5.8 49.5 %copy-start = (bf16[64,32,576]{2,1,0:T(8,128)(2,1)}, bf16[64,32,576]{2,1,0:T(8,128)(2,1)S(1)}, u32[]{:S(2)}) copy-start(bf16[64,32,576]{2,1,0:T(8,128)(2,1)S(1)} %reshape.23.q_ref) | copy-start | bytes 7077892
  55.2 16.1 %copy-start.3 = (bf16[32,512,128]{2,1,0:T(8,128)(2,1)S(1)}, bf16[32,512,128]{2,1,0:T(8,128)(2,1)}, u32[]{:S(2)}) copy-start(bf16[32,512,128]{2,1,0:T(8,128)(2,1)} %param.10) | copy-start | bytes 12582916
where the time goes:
time: 74.2 us; the launch traced here: 74.8 us
  Pallas kernels  65.5 us (88%)
  local copies, waits for them, and re-layouts  5.42 us (7%)
  matrix products  2.52 us (3%)
  other arithmetic  1.21 us (2%)
    pallas_call x1, Pallas kernels, gather_and_suffix(): pl.pallas_call(functools.partial(gather_kernel, planes, steps), in_specs=...  49.4 us
    pallas_call x1, Pallas kernels, prefix_attention(): pl.pallas_call(functools.partial(prefix_kernel, group), grid_spec=pltpu.P...  16.1 us
    reshape x1, local copies, waits for them, and re-layouts, gather_plan(): query_heads = queries.reshape(forks_here, heads_here, R + P_SIZE)  4.5 us
    dot_general x1, matrix products, project(): jnp.einsum('nhr,hrv->nhv', latent, w_uv, preferred_element_type=jnp.float32)  2.52 us

commit v1 on v0

v1 whole, which is shorter than its diff:
```python
import functools

import jax
import jax.numpy as jnp
from jax import lax
from jax.experimental import pallas as pl
from jax.experimental.pallas import tpu as pltpu
from jax.sharding import PartitionSpec as P

R = 512
P_SIZE = 64
V = 128


score_scale = 192.0 ** (-0.5)
log2e = 1.4426950408889634
OUTER = (((1,), (1,)), ((), ()))


def project(latent, w_uv):
    return jnp.einsum("nhr,hrv->nhv", latent, w_uv, preferred_element_type=jnp.float32).astype(
        jnp.bfloat16
    )


def exchange_plan(queries, prefix_cache, suffix_cache, w_uv, fork_prompt, prompt_slot, suffix_len):
    owners_count = lax.axis_size("dp")
    forks_here = queries.shape[0]
    heads_here = w_uv.shape[0]
    key_width = R + P_SIZE
    capacity = max(2, 2 * forks_here // owners_count)
    slots_all = owners_count * capacity
    prompt_ids = jnp.arange(prompt_slot.shape[0], dtype=jnp.int32)
    chosen = fork_prompt[:, 0][:, None] == prompt_ids[None, :]
    owner_slot = jnp.sum(jnp.where(chosen, prompt_slot[None, :], 0), axis=1)
    fork_order = jnp.arange(forks_here, dtype=jnp.int32)
    before = (owner_slot[:, None] == owner_slot[None, :]) & (
        fork_order[None, :] < fork_order[:, None]
    )
    slot_rank = jnp.sum(before.astype(jnp.int32), axis=1)
    target = owner_slot * capacity + slot_rank
    placing = target[None, :] == jnp.arange(slots_all, dtype=jnp.int32)[:, None]
    outbound = jnp.dot(
        placing.astype(jnp.bfloat16), queries, preferred_element_type=jnp.float32
    ).astype(jnp.bfloat16)
    outbound = outbound.reshape(owners_count, capacity, heads_here * key_width)
    gathered = lax.all_gather(prefix_cache, "tp", axis=2, tiled=True)[0]
    received = lax.all_to_all(outbound, "dp", split_axis=0, concat_axis=0, tiled=True)
    sources = received.shape[0]
    items = received.shape[1]
    lead_rows = sources * items
    query_rows = received.reshape(lead_rows * heads_here, key_width)
    scores = jnp.dot(query_rows, gathered, preferred_element_type=jnp.float32) * score_scale
    peak_score = jnp.max(scores, axis=1, keepdims=True)
    weights = jnp.exp(scores - peak_score)
    mass_sum = jnp.sum(weights, axis=1)
    summed = lax.dot_general(
        weights.astype(jnp.bfloat16),
        gathered[:R],
        (((1,), (1,)), ((), ())),
        preferred_element_type=jnp.float32,
    )
    latent = (summed / mass_sum[:, None]).astype(jnp.bfloat16)
    log_mass = (peak_score[:, 0] + jnp.log(mass_sum)).reshape(sources, items, heads_here)
    result = project(latent.reshape(lead_rows, heads_here, R), w_uv)
    result = result.reshape(sources, items, heads_here * V)
    answer, answer_mass = (
        lax.all_to_all(result, "dp", split_axis=0, concat_axis=0, tiled=True),
        lax.all_to_all(
            log_mass.astype(jnp.bfloat16), "dp", split_axis=0, concat_axis=0, tiled=True
        ).astype(log_mass.dtype),
    )
    picking = placing.astype(jnp.bfloat16)
    flat_answer = answer.reshape(slots_all, answer.shape[2])
    returned = lax.dot_general(
        picking, flat_answer, (((0,), (0,)), ((), ())), preferred_element_type=jnp.float32
    ).astype(jnp.bfloat16)
    mass_prefix = lax.dot_general(
        placing.astype(jnp.float32),
        answer_mass.reshape(slots_all, heads_here),
        (((0,), (0,)), ((), ())),
        precision=lax.Precision.HIGHEST,
    )
    value_prefix = returned.reshape(forks_here, heads_here, V)
    query_heads = queries.reshape(forks_here, heads_here, key_width)
    suffix_scores = (
        jnp.einsum("fhe,fes->fhs", query_heads, suffix_cache, preferred_element_type=jnp.float32)
        * score_scale
    )
    positions = jnp.arange(suffix_cache.shape[2], dtype=jnp.int32)
    live_mask = (positions[None, :] < suffix_len[:, None])[:, None, :]
    suffix_scores = jnp.where(live_mask, suffix_scores, -jnp.inf)
    suffix_peak = jnp.max(suffix_scores, axis=2, keepdims=True)
    suffix_weights = jnp.where(live_mask, jnp.exp(suffix_scores - suffix_peak), 0.0)
    suffix_sum = jnp.sum(suffix_weights, axis=2)
    suffix_summed = jnp.einsum(
        "fhs,frs->fhr",
        suffix_weights.astype(jnp.bfloat16),
        suffix_cache[:, :R, :],
        preferred_element_type=jnp.float32,
    )
    latent_suffix = (suffix_summed / suffix_sum[..., None]).astype(jnp.bfloat16)
    mass_suffix = suffix_peak[..., 0] + jnp.log(suffix_sum)
    value_suffix = project(latent_suffix, w_uv)
    top_mass = jnp.maximum(mass_prefix, mass_suffix)
    share_prefix = jnp.exp(mass_prefix - top_mass)[..., None]
    share_suffix = jnp.exp(mass_suffix - top_mass)[..., None]
    combined = (
        share_prefix * value_prefix.astype(jnp.float32)
        + share_suffix * value_suffix.astype(jnp.float32)
    ) / (share_prefix + share_suffix)
    return combined.astype(jnp.bfloat16).reshape(forks_here, heads_here * V)


MESH = pl.DeviceIdType.MESH
PAIR = 2 * (R + P_SIZE)
WINDOW = R + 2 * P_SIZE
TILES = WINDOW // 128
PITCH = 2 * TILES + 1


def slot_rows(owner, prompts, capacity):
    forks = owner.shape[0]
    wide = jnp.broadcast_to(owner, (forks, forks)).astype(jnp.float32)
    down = lax.broadcasted_iota(jnp.int32, (forks, forks), 0)
    across = lax.broadcasted_iota(jnp.int32, (forks, forks), 1)
    owner_row = jnp.sum(jnp.where(down == across, wide, 0.0), axis=0, keepdims=True)
    ahead = (wide == owner_row) & (down < across)
    rank = jnp.sum(jnp.where(ahead, 1.0, 0.0), axis=0, keepdims=True)
    target = (owner_row * capacity + rank).astype(jnp.int32)
    rows = lax.broadcasted_iota(jnp.int32, (prompts * capacity, forks), 0)
    return jnp.where(rows == target, 1.0, 0.0)


def stage_queries(p, q_ref, perm, staged_ref, sorted_ref):
    forks = q_ref.shape[0]
    columns = pl.ds(pl.multiple_of(p * PAIR, 128), PAIR)
    pair = q_ref[:, columns]
    sorted_ref[p] = jnp.dot(perm, pair, preferred_element_type=jnp.float32).astype(jnp.bfloat16)
    pair = pair.astype(jnp.float32)
    even = pair[:, :WINDOW]
    odd = pltpu.roll(pair[:, PAIR - WINDOW :], WINDOW - P_SIZE, 1)
    pairs = sorted_ref.shape[0]
    for b in range(forks // 8):
        for j in range(TILES):
            for half, part in enumerate((even, odd)):
                row = ((b * pairs + p) * PITCH + half * TILES + j) * 8
                staged_ref[pl.ds(pl.multiple_of(row, 8), 8), :] = part[
                    b * 8 : b * 8 + 8, j * 128 : j * 128 + 128
                ]


def suffix_chunk(first, block, pairs, lens_ref, staged_ref, cache_ref, lat_ref, mass_ref):
    width = R + P_SIZE
    heads = 2 * pairs
    pitch = heads + 8
    base = first // 8 * pairs * PITCH * 8 + first % 8
    for s in range(block):
        f = first + s
        halves = []
        for half in range(2):
            halves.append(
                jnp.concatenate(
                    [
                        staged_ref[
                            pl.ds(base + (half * TILES + j) * 8 + s, pairs, stride=PITCH * 8), :
                        ]
                        for j in range(TILES)
                    ],
                    axis=1,
                )
            )
        q = jnp.concatenate(halves, axis=0)[:, :width].astype(jnp.bfloat16)
        positions = lax.broadcasted_iota(jnp.int32, (1, cache_ref.shape[2]), 1)
        live = positions < lens_ref[f]
        scores = jnp.dot(q, cache_ref[f], preferred_element_type=jnp.float32)
        scores = jnp.where(live, scores * (score_scale * log2e), -jnp.inf)
        peak = jnp.max(scores, axis=1, keepdims=True)
        weights = jnp.exp2(scores - peak)
        mass = jnp.sum(weights, axis=1, keepdims=True)
        summed = lax.dot_general(
            weights.astype(jnp.bfloat16),
            cache_ref[f, :R, :],
            OUTER,
            preferred_element_type=jnp.float32,
        )
        latent = summed / mass
        rows = pl.ds(pl.multiple_of(f * pitch, 8), heads)
        for j in range(R // 128):
            lat_ref[j, rows, :] = latent[:, j * 128 : j * 128 + 128]
        mass_ref[rows, :] = jnp.broadcast_to(peak + jnp.log2(mass), (heads, 128))


def exact_rows(perm, value):
    high = value.astype(jnp.bfloat16)
    rest = value - high.astype(jnp.float32)
    mid = rest.astype(jnp.bfloat16)
    low = (rest - mid.astype(jnp.float32)).astype(jnp.bfloat16)
    moved = jnp.dot(
        perm, jnp.concatenate([high, mid, low], axis=1), preferred_element_type=jnp.float32
    )
    n = value.shape[1]
    return moved[:, :n] + moved[:, n : 2 * n] + moved[:, 2 * n :]


def head_of(r, pairs):
    return 2 * (r % pairs) + r // pairs


def suffix_values(r, forks, pairs, perm, lat_ref, mass_ref, w_ref, value_ref, moved_ref):
    pitch = 2 * pairs + 8
    rows = pl.ds(r, forks, stride=pitch)
    latent = jnp.concatenate([lat_ref[j, rows, :] for j in range(R // 128)], axis=1)
    value = jnp.dot(
        latent.astype(jnp.bfloat16), w_ref[head_of(r, pairs)], preferred_element_type=jnp.float32
    ).astype(jnp.bfloat16)
    value_ref[r] = jnp.dot(perm, value, preferred_element_type=jnp.float32).astype(jnp.bfloat16)
    moved_ref[r] = exact_rows(perm, mass_ref[rows, :])


def slot_attention(slot, capacity, sorted_ref, caches_ref, lat_ref, mass_ref):
    pairs = sorted_ref.shape[0]
    parts = caches_ref.shape[1]
    own = pl.ds(pl.multiple_of(slot * capacity, capacity), capacity)
    weights, masses, peaks = [], [], []
    for odd in range(2):
        first = odd * (PAIR - WINDOW)
        q = jnp.concatenate([sorted_ref[p, own, first : first + WINDOW] for p in range(pairs)], axis=0)
        keys = pl.ds((1 - odd) * P_SIZE, WINDOW)
        scores = [
            jnp.dot(q, caches_ref[slot, k, keys, :], preferred_element_type=jnp.float32)
            for k in range(parts)
        ]
        peak = functools.reduce(
            jnp.maximum, [jnp.max(piece, axis=1, keepdims=True) for piece in scores]
        )
        mass = 0.0
        pieces = []
        for k in range(parts):
            weight = jnp.exp2((scores[k] - peak) * (score_scale * log2e))
            mass = mass + jnp.sum(weight, axis=1, keepdims=True)
            pieces.append(weight.astype(jnp.bfloat16))
        weights.append(pieces)
        masses.append(mass)
        peaks.append(peak)
    summed = 0.0
    for k in range(parts):
        summed = summed + lax.dot_general(
            jnp.concatenate([weights[0][k], weights[1][k]], axis=0),
            caches_ref[slot, k, pl.ds(P_SIZE, R), :],
            OUTER,
            preferred_element_type=jnp.float32,
        )
    mass = jnp.concatenate(masses, axis=0)
    peak = jnp.concatenate(peaks, axis=0)
    latent = (summed / mass).astype(jnp.bfloat16)
    lat_ref[:, own, :] = latent.reshape(2 * pairs, capacity, R)
    log_mass = peak * (score_scale * log2e) + jnp.log2(mass)
    mass_ref[:, own, :] = jnp.broadcast_to(log_mass, (log_mass.shape[0], 128)).reshape(
        2 * pairs, capacity, 128
    )


def combine(r, pairs, lat_ref, w_ref, mass_ref, value_ref, moved_ref, out_ref):
    h = head_of(r, pairs)
    value = jnp.dot(lat_ref[r], w_ref[h], preferred_element_type=jnp.float32)
    value = value.astype(jnp.bfloat16).astype(jnp.float32)
    ours, theirs = mass_ref[r], moved_ref[r]
    top = jnp.maximum(ours, theirs)
    ours = jnp.exp2(ours - top)
    theirs = jnp.exp2(theirs - top)
    mixed = (ours * value + theirs * value_ref[r].astype(jnp.float32)) / (ours + theirs)
    out_ref[:, pl.ds(pl.multiple_of(h * 128, 128), 128)] = mixed.astype(jnp.bfloat16)


class Exchange:
    def __init__(self, caches, own, own_sem, sems):
        dp, tp = lax.axis_index("dp"), lax.axis_index("tp")
        self.planes = caches.shape[0] // 2
        self.z, self.x = dp // 2, dp % 2
        self.y, self.c = tp // 2, tp % 2
        self.caches, self.own, self.own_sem = caches, own, own_sem
        self.sems = sems
        self.low = self.z < self.planes // 2
        inward = jnp.where(self.low, self.z + 1, self.z - 1)
        outward = jnp.clip(jnp.where(self.low, self.z - 1, self.z + 1), 0, self.planes - 1)
        self.edge = (self.z == 0) | (self.z == self.planes - 1)
        self.to = dict(
            x=(self.z * 2 + 1 - self.x, tp),
            y=(dp, (1 - self.y) * 2 + self.c),
            pair=(dp, self.y * 2 + 1 - self.c),
            inward=(inward * 2 + self.x, tp),
            outward=(outward * 2 + self.x, tp),
        )
        self.rows = own.shape[1]
        self.pad = (caches.shape[2] - self.rows) // 2

    def plane(self, q):
        return jnp.where(self.low, q, self.planes - 1 - q)

    def place(self, q, far_x=0, far_y=0, half=None):
        xx = 1 - self.x if far_x else self.x
        yy = 1 - self.y if far_y else self.y
        first, count = self.pad, self.rows
        if half is not None:
            count = self.rows // 2
            first = first + half * count
        return self.caches.at[self.plane(q) * 2 + xx, yy * 2 + self.c, pl.ds(first, count)]

    def copy(self, kind, q, half, sender):
        far_x, far_y, index = {
            "u": (0, 0, 0),
            "d": (1, 1, 1),
            "x": (0, 0, 2),
            "y": (0, 0, 3),
            "dx": (0, 1, 4),
            "dy": (1, 0, 4),
        }[kind]
        link = {"x": "x", "dx": "x", "y": "y", "dy": "y"}.get(kind, sender)
        sends = {"inward": 0, "outward": 2, "x": 4, "y": 5, "dx": 6, "dy": 6}
        send = sends[sender] + (kind == "d") if kind in ("u", "d") else sends[kind]
        part = self.place(q, far_x, far_y, half)
        zz = self.plane(q)
        send_sem, recv_sem = self.sems["send"], self.sems["recv"]
        return pltpu.make_async_remote_copy(
            src_ref=part,
            dst_ref=part,
            send_sem=send_sem.at[send, zz, half],
            recv_sem=recv_sem.at[index, zz, half],
            device_id=self.to[link],
            device_id_type=MESH,
        )

    def send(self, kind, q, half, sender=None):
        self.copy(kind, q, half, sender).start()
        self.sent.append((kind, q, half, sender))

    def got(self, kind, q, half):
        self.copy(kind, q, half, "inward").wait_recv()

    def pair(self, q, far_x, far_y):
        part = self.place(q, far_x, far_y)
        xx = 1 - self.x if far_x else self.x
        yy = 1 - self.y if far_y else self.y
        k = (self.plane(q) * 2 + xx) * 2 + yy
        return pltpu.make_async_remote_copy(
            src_ref=part,
            dst_ref=part,
            send_sem=self.sems["pair_send"].at[k],
            recv_sem=self.sems["pair_recv"].at[k],
            device_id=self.to["pair"],
            device_id_type=MESH,
        )

    def load(self):
        return pltpu.make_async_copy(self.own.at[0], self.place_own(), self.own_sem)

    def place_own(self):
        slot = self.z * 2 + self.x
        return self.caches.at[slot, self.y * 2 + self.c, pl.ds(self.pad, self.rows)]

    def barrier(self):
        sem = pltpu.get_barrier_semaphore()
        for name in ("x", "y", "pair", "inward"):
            pl.semaphore_signal(sem, inc=1, device_id=self.to[name], device_id_type=MESH)

        @pl.when(~self.edge)
        def _():
            pl.semaphore_signal(sem, inc=1, device_id=self.to["outward"], device_id_type=MESH)

        pl.semaphore_wait(sem, jnp.where(self.edge, 4, 5))

    def rounds(self, edge):
        send, got = self.send, self.got
        self.sent = []

        def first():
            q = 0 if edge else 1
            for half in range(2):
                send("u", q, half, "inward")
                if not edge:
                    send("u", q, half, "outward")
                send("x", q, half)
                send("y", q, 1 - half)
            self.pair(q, 0, 0).start()

        def both(kind, q):
            got(kind, q, 0)
            got(kind, q, 1)

        def sides(q):
            both("x", q)
            self.pair(q, 1, 0).start()
            both("y", q)
            self.pair(q, 0, 1).start()

        def sides_late(q):
            got("x", q, 1)
            self.pair(q, 1, 0).start()
            got("y", q, 0)
            self.pair(q, 0, 1).start()

        def cross(q):
            got("x", q, 0)
            send("dy", q, 0)
            got("y", q, 1)
            send("dx", q, 1)

        def crossed(q):
            got("dy", q, 0)
            got("dx", q, 1)
            self.pair(q, 1, 1).start()

        def diagonal(q):
            both("d", q)
            self.pair(q, 1, 1).start()

        def e1():
            cross(0)
            got("u", 1, 0)
            send("x", 1, 0)
            send("y", 1, 0)

        def e2():
            got("u", 1, 1)
            send("x", 1, 1)
            send("y", 1, 1)
            self.pair(1, 0, 0).start()
            sides_late(0)

        def e3():
            crossed(0)
            got("u", 2, 0)
            send("x", 2, 0)
            send("y", 2, 0)

        def e4():
            got("u", 2, 1)
            send("x", 2, 1)
            send("y", 2, 1)
            self.pair(2, 0, 0).start()

        def e5():
            sides(1)
            got("u", 3, 0)
            send("x", 3, 0)

        def e6():
            got("u", 3, 1)
            send("y", 3, 1)
            send("y", 3, 0)
            send("x", 3, 1)
            self.pair(3, 0, 0).start()

        def e7():
            sides(2)

        def e8():
            cross(3)
            diagonal(1)

        def e9():
            sides_late(3)

        def e10():
            crossed(3)
            diagonal(2)

        def i1():
            cross(1)
            got("u", 2, 0)
            send("u", 2, 0, "outward")
            got("u", 0, 0)
            send("u", 0, 0, "inward")
            send("x", 0, 0)

        def i2():
            got("u", 2, 1)
            send("u", 2, 1, "outward")
            got("u", 0, 1)
            send("u", 0, 1, "inward")
            send("y", 0, 1)
            send("y", 0, 0)
            send("x", 0, 1)
            self.pair(2, 0, 0).start()
            self.pair(0, 0, 0).start()
            sides_late(1)

        def i3():
            crossed(1)
            for half in range(2):
                send("d", 1, half, "inward")
            got("u", 3, 0)
            send("u", 3, 0, "outward")

        def i4():
            got("u", 3, 1)
            send("u", 3, 1, "outward")
            self.pair(3, 0, 0).start()
            for half in range(2):
                send("d", 1, half, "outward")
            cross(0)
            for q in (2, 3):
                for half in range(2):
                    send("x", q, half)
                    send("y", q, half)

        def i5():
            sides_late(0)

        def i6():
            crossed(0)
            for half in range(2):
                send("d", 0, half, "inward")
            for half in range(2):
                got("d", 2, half)
                send("d", 2, half, "outward")
            self.pair(2, 1, 1).start()

        def i7():
            pass

        def i8():
            sides(2)

        def i9():
            diagonal(3)

        def i10():
            sides(3)

        if edge:
            return [first, e1, e2, e3, e4, e5, e6, e7, e8, e9, e10]
        return [first, i1, i2, i3, i4, i5, i6, i7, i8, i9, i10]

    def round(self, r):
        edge = []
        for side, when in ((True, self.edge), (False, ~self.edge)):
            @pl.when(when)
            def _(side=side):
                self.rounds(side)[r]()
            edge.append(self.sent)
        self.all_sent = getattr(self, "all_sent", [])
        self.all_sent.append(edge)

    def finish(self):
        for side, when in ((0, self.edge), (1, ~self.edge)):
            @pl.when(when)
            def _(side=side):
                for sent in self.all_sent:
                    for item in sent[side]:
                        self.copy(*item).wait_send()
        for k in range(2 * self.caches.shape[0]):
            pltpu.make_async_remote_copy(
                src_ref=self.place_own(), dst_ref=self.place_own(),
                send_sem=self.sems["pair_send"].at[k], recv_sem=self.sems["pair_recv"].at[k],
                device_id=self.to["pair"], device_id_type=MESH).wait_send()

    def pair_done(self, slot, y):
        pltpu.make_async_remote_copy(
            src_ref=self.place_own(), dst_ref=self.place_own(),
            send_sem=self.sems["pair_send"].at[slot * 2 + y], recv_sem=self.sems["pair_recv"].at[slot * 2 + y],
            device_id=self.to["pair"], device_id_type=MESH).wait_recv()


def pick(table, index):
    value = table[-1]
    for i in range(len(table) - 2, -1, -1):
        value = jnp.where(index == i, table[i], value)
    return value


EDGE_SLOTS = ((0, 0), (0, 1), (1, 0), (2, 0), (1, 1), (3, 0), (2, 1), (3, 1))
INNER_SLOTS = ((1, 0), (1, 1), (0, 0), (0, 1), (2, 0), (2, 1), (3, 0), (3, 1))
PLAN = ("hh", "hhh", "hhh", "ah", "ahh", "hah", "hhh", "avvv", "avvv", "avv", "aa")


def fused_kernel(
    slot_ref,
    lens_ref,
    prompt_ref,
    own,
    q_hbm,
    suffix_hbm,
    w_hbm,
    out_ref,
    perm_ref,
    caches,
    held,
    q_ref,
    staged,
    placed,
    w_ref,
    suffix_lat,
    suffix_mass,
    suffix_value,
    moved_mass,
    lat,
    mass,
    load_sems,
    own_sem,
    send_sems,
    recv_sems,
    pair_send,
    pair_recv,
):
    forks = q_ref.shape[0]
    pairs = placed.shape[0]
    slots = caches.shape[0]
    capacity = placed.shape[1] // slots
    exchange = Exchange(
        caches,
        own,
        own_sem,
        dict(send=send_sems, recv=recv_sems, pair_send=pair_send, pair_recv=pair_recv),
    )
    exchange.load().start()
    sources = ((q_hbm, q_ref), (suffix_hbm, held), (w_hbm, w_ref))
    loads = [pltpu.make_async_copy(a, b, load_sems.at[i]) for i, (a, b) in enumerate(sources)]
    loads[0].start()
    exchange.barrier()
    exchange.load().wait()
    exchange.round(0)
    loads[1].start()
    loads[2].start()

    pad = jnp.zeros((caches.shape[1], P_SIZE, caches.shape[3]), jnp.bfloat16)

    def clear(s, carry):
        caches[s, :, :P_SIZE, :] = pad
        caches[s, :, P_SIZE + R + P_SIZE :, :] = pad
        return carry

    lax.fori_loop(0, slots, clear, 0)
    owner = jnp.zeros(prompt_ref.shape, jnp.int32)
    for p in range(slot_ref.shape[0]):
        owner = jnp.where(prompt_ref[...] == p, slot_ref[p], owner)
    perm_ref[...] = slot_rows(owner, slots, capacity).astype(jnp.bfloat16)
    loads[0].wait()

    def stage(p, carry):
        stage_queries(p, q_ref, perm_ref[...], staged, placed)
        return carry

    lax.fori_loop(0, pairs, stage, 0)
    loads[1].wait()
    loads[2].wait()

    kinds = "".join(PLAN)
    count = {kind: kinds.count(kind) for kind in "hav"}
    before = {
        kind: [kinds[:k].count(kind) for k in range(len(kinds))] for kind in "hav"
    }
    starts = [sum(len(part) for part in PLAN[:r]) for r in range(len(PLAN))]
    block = forks // count["h"]
    group = 2 * pairs // count["v"]

    def is_kind(k, kind):
        hit = k < 0
        for i, name in enumerate(kinds):
            if name == kind:
                hit = hit | (k == i)
        return hit

    def step(k, carry):
        for r in range(1, len(PLAN)):
            @pl.when(k == starts[r])
            def _(r=r):
                exchange.round(r)

        @pl.when(is_kind(k, "h"))
        def _():
            first = pick(before["h"], k) * block
            suffix_chunk(first, block, pairs, lens_ref, staged, held, suffix_lat, suffix_mass)

        @pl.when(is_kind(k, "a"))
        def _():
            n = pick(before["a"], k)
            q = jnp.where(
                exchange.edge, pick([s[0] for s in EDGE_SLOTS], n), pick([s[0] for s in INNER_SLOTS], n)
            )
            far = jnp.where(
                exchange.edge, pick([s[1] for s in EDGE_SLOTS], n), pick([s[1] for s in INNER_SLOTS], n)
            )
            xx = jnp.where(far == 1, 1 - exchange.x, exchange.x)
            slot = exchange.plane(q) * 2 + xx
            exchange.pair_done(slot, 0)
            exchange.pair_done(slot, 1)
            slot_attention(slot, capacity, placed, caches, lat, mass)

        @pl.when(is_kind(k, "v"))
        def _():
            first = pick(before["v"], k) * group
            for i in range(group):
                suffix_values(
                    first + i, forks, pairs, perm_ref[...], suffix_lat, suffix_mass, w_ref,
                    suffix_value, moved_mass,
                )

        return carry

    lax.fori_loop(0, len(kinds), step, 0)

    def finish(r, carry):
        for i in range(4):
            combine(4 * r + i, pairs, lat, w_ref, mass, suffix_value, moved_mass, out_ref)
        return carry

    lax.fori_loop(0, 2 * pairs // 4, finish, 0)
    exchange.finish()


def fused(queries, prefix_cache, suffix_cache, w_uv, fork_prompt, prompt_slot, suffix_len):
    forks, columns = queries.shape
    heads = w_uv.shape[0]
    pairs = heads // 2
    slots, parts = lax.axis_size("dp"), lax.axis_size("tp")
    planes = slots // 2
    rows = slots * slot_capacity(forks, slots)
    keys = prefix_cache.shape[2]
    pitch = heads + 8
    dma = pltpu.SemaphoreType.DMA
    vmem = pl.BlockSpec(memory_space=pltpu.VMEM)
    smem = pl.BlockSpec(memory_space=pltpu.SMEM)
    hbm = pl.BlockSpec(memory_space=pl.ANY)
    bf16, f32 = jnp.bfloat16, jnp.float32
    return pl.pallas_call(
        fused_kernel,
        in_specs=[smem, smem, vmem, hbm, hbm, hbm, hbm],
        out_specs=[vmem, vmem],
        out_shape=[
            jax.ShapeDtypeStruct((rows, heads * V), bf16),
            jax.ShapeDtypeStruct((rows, forks), bf16),
        ],
        scratch_shapes=[
            pltpu.VMEM((slots, parts, R + 3 * P_SIZE, keys), bf16),
            pltpu.VMEM(suffix_cache.shape, bf16),
            pltpu.VMEM((forks, columns), bf16),
            pltpu.VMEM((forks * pairs * PITCH, 128), f32),
            pltpu.VMEM((pairs, rows, PAIR), bf16),
            pltpu.VMEM(w_uv.shape, bf16),
            pltpu.VMEM((R // 128, forks * pitch, 128), f32),
            pltpu.VMEM((forks * pitch, 128), f32),
            pltpu.VMEM((heads, rows, V), bf16),
            pltpu.VMEM((heads, rows, 128), f32),
            pltpu.VMEM((heads, rows, R), bf16),
            pltpu.VMEM((heads, rows, 128), f32),
            dma((3,)),
            dma,
            dma((7, planes, 2)),
            dma((5, planes, 2)),
            dma((slots * 2,)),
            dma((slots * 2,)),
        ],
        compiler_params=pltpu.CompilerParams(
            collective_id=0, has_side_effects=True, vmem_limit_bytes=67043328
        ),
        name="fused",
    )(prompt_slot, suffix_len, fork_prompt, prefix_cache, queries, suffix_cache, w_uv)


def slot_capacity(forks, slots):
    return max(2, 2 * forks // slots)


def gather_plan(*args):
    mixed, placing = fused(*args)
    return lax.dot_general(
        placing, mixed, (((0,), (0,)), ((), ())), preferred_element_type=jnp.float32
    ).astype(jnp.bfloat16)


def shards(queries, prefix_cache, *others):
    owners_count = lax.axis_size("dp")
    forks_here = queries.shape[0]
    capacity = max(2, 2 * forks_here // owners_count)
    sent = owners_count * capacity * queries.shape[1]
    gathered = owners_count * lax.axis_size("tp") * prefix_cache.size
    square = lax.axis_size("tp") == 4 and owners_count == 2 * len(EDGE_SLOTS) // 2
    plan = gather_plan if square and gathered <= 4 * sent else exchange_plan
    return plan(queries, prefix_cache, *others)


def solution(mesh):
    placed = (
        P("dp", "tp"),
        P("dp", None, "tp"),
        P("dp", None, None),
        P("tp", None, None),
        P("dp", None),
        P(),
        P("dp"),
    )
    return jax.shard_map(
        shards, mesh=mesh, in_specs=placed, out_specs=P("dp", "tp"), check_vma=False
    )
```

time: 74.2 us -> 66.5 us (0.90); the launches traced: 74.8 us -> 66.2 us
  local copies, waits for them, and re-layouts: 5.42 us -> 1.36 us
  Pallas kernels: 65.5 us -> 62.4 us
  other arithmetic: 1.21 us -> 0 us
    reshape x2 -> x0, local copies, waits for them, and re-layouts: 5.4 us -> none  [the longest x1 4.5 us: gather_plan(): query_heads = queries.reshape(forks_here, heads_here, R + P_SIZE)]
    pallas_call x2 -> x1, Pallas kernels: 65.5 us -> 62.4 us  [fused(): pl.pallas_call(fused_kernel, in_specs=[smem, smem, vmem, hbm, hbm, hbm, h...]
    unnamed x8 -> x1, local copies, waits for them, and re-layouts: 0.02 us -> 1.36 us
    reduce_sum x4 -> x0, other arithmetic: 1.2 us -> none  [the longest x1 0.8 us: fork_order(): owner_slot = jnp.sum(jnp.where(chosen, prompt_slot[None, :], 0), axis=1)]
where the time goes in v1:
time: 66.5 us; the launch traced here: 66.2 us
  Pallas kernels  62.4 us (94%)
  matrix products  2.37 us (4%)
  local copies, waits for them, and re-layouts  1.36 us (2%)
    pallas_call x1, Pallas kernels, fused(): pl.pallas_call(fused_kernel, in_specs=[smem, smem, vmem, hbm, hbm, hbm, h...  62.4 us
    dot_general x1, matrix products, gather_plan(): lax.dot_general(placing, mixed, (((0,), (0,)), ((), ())), preferred_eleme...  2.37 us
    unnamed x1, local copies, waits for them, and re-layouts  1.36 us

profile of v1, /device:TPU:0, one launch (start us, length us, event | category | flops | bytes accessed | tf_op | source)
XLA Modules:
  0.0 66.2 jit_solution(7016057171885597820)
XLA Ops:
  0.0 1.4 %copy.8.prompt_ref = s32[64,1]{1,0:T(8,128)} copy(s32[64,1]{0,1:T(1,128)} %param.11) | data formatting | bytes 512 | tf_op args[4]
  1.4 62.4 %fused.1 = (bf16[128,4096]{1,0:T(8,128)(2,1)}, bf16[128,64]{1,0:T(8,128)(2,1)}) custom-call(s32[8]{0:T(128)} %slot_ref.1, s32[64]{0:T(128)} %lens_ref.1, s32[64,1]{1,0:T(8,128)} %copy.8.prompt_ref, bf16[1,576,256]{2,1,0:T(8,128)(2,1)} %own.1, bf16[64,18432]{1,0:T(8,128)(2,1)} %q_hbm.1, bf16[64,576,128]{2,1,0:T(8,128)(2,1)} %suffix_hbm.1, ...), custom_call_target="tpu_custom_call" | custom-call | tf_op jit(solution)/shard_map/fused/pallas_call | solution.py:727
  63.8 2.4 %convolution_convert_fusion = bf16[64,4096]{1,0:T(8,128)(2,1)} fusion(bf16[128,64]{1,0:T(8,128)(2,1)} %get-tuple-element.7, bf16[128,4096]{1,0:T(8,128)(2,1)} %get-tuple-element.8), kind=kOutput, calls=%fused_computation | convolution fusion | flops 67371008 | bytes 1589248 | tf_op jit(solution)/shard_map/dot_general | solution.py:768

commit v2 on v1

--- a/solution.py
+++ b/solution.py
@@ -119,31 +119,32 @@
 PITCH = 2 * TILES + 1
 
 
-def slot_rows(owner, prompts, capacity):
-    forks = owner.shape[0]
-    wide = jnp.broadcast_to(owner, (forks, forks)).astype(jnp.float32)
+def slot_rows(owner, slots, capacity):
+    forks = owner.shape[1]
     down = lax.broadcasted_iota(jnp.int32, (forks, forks), 0)
     across = lax.broadcasted_iota(jnp.int32, (forks, forks), 1)
-    owner_row = jnp.sum(jnp.where(down == across, wide, 0.0), axis=0, keepdims=True)
-    ahead = (wide == owner_row) & (down < across)
+    wide = jnp.broadcast_to(owner, (forks, forks))
+    column = jnp.sum(jnp.where(down == across, wide, 0.0), axis=1, keepdims=True)
+    ahead = (column == wide) & (down < across)
     rank = jnp.sum(jnp.where(ahead, 1.0, 0.0), axis=0, keepdims=True)
-    target = (owner_row * capacity + rank).astype(jnp.int32)
-    rows = lax.broadcasted_iota(jnp.int32, (prompts * capacity, forks), 0)
+    target = (owner * capacity + rank).astype(jnp.int32)
+    rows = lax.broadcasted_iota(jnp.int32, (slots * capacity, forks), 0)
     return jnp.where(rows == target, 1.0, 0.0)
 
 
-def stage_queries(p, q_ref, perm, staged_ref, sorted_ref):
+def stage_queries(p, q_ref, perm, staged_ref, placed_ref):
     forks = q_ref.shape[0]
     columns = pl.ds(pl.multiple_of(p * PAIR, 128), PAIR)
-    pair = q_ref[:, columns]
-    sorted_ref[p] = jnp.dot(perm, pair, preferred_element_type=jnp.float32).astype(jnp.bfloat16)
-    pair = pair.astype(jnp.float32)
+    pair = q_ref[:, columns].astype(jnp.float32)
     even = pair[:, :WINDOW]
     odd = pltpu.roll(pair[:, PAIR - WINDOW :], WINDOW - P_SIZE, 1)
-    pairs = sorted_ref.shape[0]
-    for b in range(forks // 8):
-        for j in range(TILES):
-            for half, part in enumerate((even, odd)):
+    pairs = placed_ref.shape[1]
+    for half, part in enumerate((even, odd)):
+        placed_ref[half, p] = jnp.dot(
+            perm, part.astype(jnp.bfloat16), preferred_element_type=jnp.float32
+        ).astype(jnp.bfloat16)
+        for b in range(forks // 8):
+            for j in range(TILES):
                 row = ((b * pairs + p) * PITCH + half * TILES + j) * 8
                 staged_ref[pl.ds(pl.multiple_of(row, 8), 8), :] = part[
                     b * 8 : b * 8 + 8, j * 128 : j * 128 + 128
@@ -151,56 +152,63 @@
 
 
 def suffix_chunk(first, block, pairs, lens_ref, staged_ref, cache_ref, lat_ref, mass_ref):
-    width = R + P_SIZE
     heads = 2 * pairs
     pitch = heads + 8
+    keys = cache_ref.shape[2]
     base = first // 8 * pairs * PITCH * 8 + first % 8
-    for s in range(block):
-        f = first + s
-        halves = []
-        for half in range(2):
-            halves.append(
-                jnp.concatenate(
-                    [
-                        staged_ref[
-                            pl.ds(base + (half * TILES + j) * 8 + s, pairs, stride=PITCH * 8), :
-                        ]
-                        for j in range(TILES)
-                    ],
-                    axis=1,
+    positions = lax.broadcasted_iota(jnp.int32, (1, keys), 1)
+    batch = 128 // heads
+    for start in range(0, block, batch):
+        masses, latents, weights = [], [], []
+        for i in range(batch):
+            s = start + i
+            f = first + s
+            halves = []
+            for half in range(2):
+                halves.append(
+                    jnp.concatenate(
+                        [
+                            staged_ref[
+                                pl.ds(base + (half * TILES + j) * 8 + s, pairs, stride=PITCH * 8), :
+                            ]
+                            for j in range(TILES)
+                        ],
+                        axis=1,
+                    )
                 )
-            )
-        q = jnp.concatenate(halves, axis=0)[:, :width].astype(jnp.bfloat16)
-        positions = lax.broadcasted_iota(jnp.int32, (1, cache_ref.shape[2]), 1)
-        live = positions < lens_ref[f]
-        scores = jnp.dot(q, cache_ref[f], preferred_element_type=jnp.float32)
-        scores = jnp.where(live, scores * (score_scale * log2e), -jnp.inf)
-        peak = jnp.max(scores, axis=1, keepdims=True)
-        weights = jnp.exp2(scores - peak)
-        mass = jnp.sum(weights, axis=1, keepdims=True)
+            q = jnp.concatenate(halves, axis=0)[:, : R + P_SIZE].astype(jnp.bfloat16)
+            scores = jnp.dot(q, cache_ref[f], preferred_element_type=jnp.float32)
+            live = positions < lens_ref[f]
+            scores = jnp.where(live, scores * (score_scale * log2e), -jnp.inf)
+            peak = jnp.max(scores, axis=1, keepdims=True)
+            weight = jnp.exp2(scores - peak)
+            mass = jnp.sum(weight, axis=1, keepdims=True)
+            rows = pl.ds(pl.multiple_of(f * pitch, 8), heads)
+            mass_ref[rows, :] = jnp.broadcast_to(peak + jnp.log2(mass), (heads, 128))
+            masses.append(mass)
+            latents.append(cache_ref[f, :R, :])
+            blocks = [jnp.zeros((heads, keys), jnp.bfloat16)] * batch
+            blocks[i] = weight.astype(jnp.bfloat16)
+            weights.append(jnp.concatenate(blocks, axis=0))
         summed = lax.dot_general(
-            weights.astype(jnp.bfloat16),
-            cache_ref[f, :R, :],
+            jnp.concatenate(latents, axis=1),
+            jnp.concatenate(weights, axis=1),
             OUTER,
             preferred_element_type=jnp.float32,
         )
-        latent = summed / mass
-        rows = pl.ds(pl.multiple_of(f * pitch, 8), heads)
-        for j in range(R // 128):
-            lat_ref[j, rows, :] = latent[:, j * 128 : j * 128 + 128]
-        mass_ref[rows, :] = jnp.broadcast_to(peak + jnp.log2(mass), (heads, 128))
-
-
-def exact_rows(perm, value):
+        latent = summed.T / jnp.concatenate(masses, axis=0)
+        for i in range(batch):
+            rows = pl.ds(pl.multiple_of((first + start + i) * pitch, 8), heads)
+            for j in range(R // 128):
+                lat_ref[j, rows, :] = latent[i * heads : (i + 1) * heads, j * 128 : j * 128 + 128]
+
+
+def in_parts(value):
     high = value.astype(jnp.bfloat16)
     rest = value - high.astype(jnp.float32)
     mid = rest.astype(jnp.bfloat16)
     low = (rest - mid.astype(jnp.float32)).astype(jnp.bfloat16)
-    moved = jnp.dot(
-        perm, jnp.concatenate([high, mid, low], axis=1), preferred_element_type=jnp.float32
-    )
-    n = value.shape[1]
-    return moved[:, :n] + moved[:, n : 2 * n] + moved[:, 2 * n :]
+    return jnp.concatenate([high, mid, low], axis=0)
 
 
 def head_of(r, pairs):
@@ -214,45 +222,39 @@
     value = jnp.dot(
         latent.astype(jnp.bfloat16), w_ref[head_of(r, pairs)], preferred_element_type=jnp.float32
     ).astype(jnp.bfloat16)
-    value_ref[r] = jnp.dot(perm, value, preferred_element_type=jnp.float32).astype(jnp.bfloat16)
-    moved_ref[r] = exact_rows(perm, mass_ref[rows, :])
-
-
-def slot_attention(slot, capacity, sorted_ref, caches_ref, lat_ref, mass_ref):
-    pairs = sorted_ref.shape[0]
+    none = jnp.zeros((2 * forks, V), jnp.bfloat16)
+    both = jnp.concatenate(
+        [jnp.concatenate([value, none], axis=0), in_parts(mass_ref[rows, :])], axis=1
+    )
+    moved = jnp.dot(perm, both, preferred_element_type=jnp.float32)
+    value_ref[r] = moved[:, :V].astype(jnp.bfloat16)
+    moved_ref[r] = moved[:, V:]
+
+
+def slot_attention(slot, capacity, placed_ref, caches_ref, lat_ref, mass_ref):
+    pairs = placed_ref.shape[1]
     parts = caches_ref.shape[1]
     own = pl.ds(pl.multiple_of(slot * capacity, capacity), capacity)
-    weights, masses, peaks = [], [], []
-    for odd in range(2):
-        first = odd * (PAIR - WINDOW)
-        q = jnp.concatenate([sorted_ref[p, own, first : first + WINDOW] for p in range(pairs)], axis=0)
-        keys = pl.ds((1 - odd) * P_SIZE, WINDOW)
-        scores = [
-            jnp.dot(q, caches_ref[slot, k, keys, :], preferred_element_type=jnp.float32)
-            for k in range(parts)
-        ]
-        peak = functools.reduce(
-            jnp.maximum, [jnp.max(piece, axis=1, keepdims=True) for piece in scores]
-        )
-        mass = 0.0
-        pieces = []
-        for k in range(parts):
-            weight = jnp.exp2((scores[k] - peak) * (score_scale * log2e))
-            mass = mass + jnp.sum(weight, axis=1, keepdims=True)
-            pieces.append(weight.astype(jnp.bfloat16))
-        weights.append(pieces)
-        masses.append(mass)
-        peaks.append(peak)
+    q = jnp.concatenate(
+        [placed_ref[half, p, own, :] for half in range(2) for p in range(pairs)], axis=0
+    )
+    scores = [
+        jnp.dot(q, caches_ref[slot, k], preferred_element_type=jnp.float32) for k in range(parts)
+    ]
+    peak = functools.reduce(
+        jnp.maximum, [jnp.max(piece, axis=1, keepdims=True) for piece in scores]
+    )
+    mass = 0.0
     summed = 0.0
     for k in range(parts):
+        weight = jnp.exp2((scores[k] - peak) * (score_scale * log2e))
+        mass = mass + jnp.sum(weight, axis=1, keepdims=True)
         summed = summed + lax.dot_general(
-            jnp.concatenate([weights[0][k], weights[1][k]], axis=0),
-            caches_ref[slot, k, pl.ds(P_SIZE, R), :],
+            weight.astype(jnp.bfloat16),
+            caches_ref[slot, k, :R, :],
             OUTER,
             preferred_element_type=jnp.float32,
         )
-    mass = jnp.concatenate(masses, axis=0)
-    peak = jnp.concatenate(peaks, axis=0)
     latent = (summed / mass).astype(jnp.bfloat16)
     lat_ref[:, own, :] = latent.reshape(2 * pairs, capacity, R)
     log_mass = peak * (score_scale * log2e) + jnp.log2(mass)
@@ -293,7 +295,6 @@
             outward=(outward * 2 + self.x, tp),
         )
         self.rows = own.shape[1]
-        self.pad = (caches.shape[2] - self.rows) // 2
 
     def plane(self, q):
         return jnp.where(self.low, q, self.planes - 1 - q)
@@ -301,10 +302,10 @@
     def place(self, q, far_x=0, far_y=0, half=None):
         xx = 1 - self.x if far_x else self.x
         yy = 1 - self.y if far_y else self.y
-        first, count = self.pad, self.rows
+        first, count = 0, self.rows
         if half is not None:
             count = self.rows // 2
-            first = first + half * count
+            first = half * count
         return self.caches.at[self.plane(q) * 2 + xx, yy * 2 + self.c, pl.ds(first, count)]
 
     def copy(self, kind, q, half, sender):
@@ -357,7 +358,7 @@
 
     def place_own(self):
         slot = self.z * 2 + self.x
-        return self.caches.at[slot, self.y * 2 + self.c, pl.ds(self.pad, self.rows)]
+        return self.caches.at[slot, self.y * 2 + self.c, pl.ds(0, self.rows)]
 
     def barrier(self):
         sem = pltpu.get_barrier_semaphore()
@@ -572,7 +573,7 @@
 
 EDGE_SLOTS = ((0, 0), (0, 1), (1, 0), (2, 0), (1, 1), (3, 0), (2, 1), (3, 1))
 INNER_SLOTS = ((1, 0), (1, 1), (0, 0), (0, 1), (2, 0), (2, 1), (3, 0), (3, 1))
-PLAN = ("hh", "hhh", "hhh", "ah", "ahh", "hah", "hhh", "avvv", "avvv", "avv", "aa")
+PLAN = ("h", "hhh", "hhh", "ah", "avv", "vvva", "vvv", "a", "a", "a", "aa")
 
 
 def fused_kernel(
@@ -584,6 +585,7 @@
     suffix_hbm,
     w_hbm,
     out_ref,
+    mixed_ref,
     perm_ref,
     caches,
     held,
@@ -605,9 +607,9 @@
     pair_recv,
 ):
     forks = q_ref.shape[0]
-    pairs = placed.shape[0]
+    pairs = placed.shape[1]
     slots = caches.shape[0]
-    capacity = placed.shape[1] // slots
+    capacity = placed.shape[2] // slots
     exchange = Exchange(
         caches,
         own,
@@ -627,14 +629,13 @@
     pad = jnp.zeros((caches.shape[1], P_SIZE, caches.shape[3]), jnp.bfloat16)
 
     def clear(s, carry):
-        caches[s, :, :P_SIZE, :] = pad
-        caches[s, :, P_SIZE + R + P_SIZE :, :] = pad
+        caches[s, :, R + P_SIZE :, :] = pad
         return carry
 
     lax.fori_loop(0, slots, clear, 0)
-    owner = jnp.zeros(prompt_ref.shape, jnp.int32)
+    owner = jnp.zeros(prompt_ref.shape, jnp.float32)
     for p in range(slot_ref.shape[0]):
-        owner = jnp.where(prompt_ref[...] == p, slot_ref[p], owner)
+        owner = jnp.where(prompt_ref[...] == p, slot_ref[p].astype(jnp.float32), owner)
     perm_ref[...] = slot_rows(owner, slots, capacity).astype(jnp.bfloat16)
     loads[0].wait()
 
@@ -691,9 +692,11 @@
         @pl.when(is_kind(k, "v"))
         def _():
             first = pick(before["v"], k) * group
+            perm = perm_ref[...]
+            perm = jnp.concatenate([perm, perm, perm], axis=1)
             for i in range(group):
                 suffix_values(
-                    first + i, forks, pairs, perm_ref[...], suffix_lat, suffix_mass, w_ref,
+                    first + i, forks, pairs, perm, suffix_lat, suffix_mass, w_ref,
                     suffix_value, moved_mass,
                 )
 
@@ -702,11 +705,16 @@
     lax.fori_loop(0, len(kinds), step, 0)
 
     def finish(r, carry):
-        for i in range(4):
-            combine(4 * r + i, pairs, lat, w_ref, mass, suffix_value, moved_mass, out_ref)
+        for i in range(8):
+            combine(8 * r + i, pairs, lat, w_ref, mass, suffix_value, moved_mass, mixed_ref)
         return carry
 
-    lax.fori_loop(0, 2 * pairs // 4, finish, 0)
+    lax.fori_loop(0, 2 * pairs // 8, finish, 0)
+    perm = perm_ref[...]
+    for j in range(0, out_ref.shape[1], 256):
+        out_ref[:, j : j + 256] = lax.dot_general(
+            perm, mixed_ref[:, j : j + 256], (((0,), (0,)), ((), ())), preferred_element_type=jnp.float32
+        ).astype(jnp.bfloat16)
     exchange.finish()
 
 
@@ -727,17 +735,16 @@
     return pl.pallas_call(
         fused_kernel,
         in_specs=[smem, smem, vmem, hbm, hbm, hbm, hbm],
-        out_specs=[vmem, vmem],
-        out_shape=[
-            jax.ShapeDtypeStruct((rows, heads * V), bf16),
-            jax.ShapeDtypeStruct((rows, forks), bf16),
-        ],
+        out_specs=vmem,
+        out_shape=jax.ShapeDtypeStruct((forks, heads * V), bf16),
         scratch_shapes=[
-            pltpu.VMEM((slots, parts, R + 3 * P_SIZE, keys), bf16),
+            pltpu.VMEM((rows, heads * V), bf16),
+            pltpu.VMEM((rows, forks), bf16),
+            pltpu.VMEM((slots, parts, WINDOW, keys), bf16),
             pltpu.VMEM(suffix_cache.shape, bf16),
             pltpu.VMEM((forks, columns), bf16),
             pltpu.VMEM((forks * pairs * PITCH, 128), f32),
-            pltpu.VMEM((pairs, rows, PAIR), bf16),
+            pltpu.VMEM((2, pairs, rows, WINDOW), bf16),
             pltpu.VMEM(w_uv.shape, bf16),
             pltpu.VMEM((R // 128, forks * pitch, 128), f32),
             pltpu.VMEM((forks * pitch, 128), f32),
@@ -756,7 +763,7 @@
             collective_id=0, has_side_effects=True, vmem_limit_bytes=67043328
         ),
         name="fused",
-    )(prompt_slot, suffix_len, fork_prompt, prefix_cache, queries, suffix_cache, w_uv)
+    )(prompt_slot, suffix_len, fork_prompt.reshape(1, forks), prefix_cache, queries, suffix_cache, w_uv)
 
 
 def slot_capacity(forks, slots):
@@ -764,10 +771,7 @@
 
 
 def gather_plan(*args):
-    mixed, placing = fused(*args)
-    return lax.dot_general(
-        placing, mixed, (((0,), (0,)), ((), ())), preferred_element_type=jnp.float32
-    ).astype(jnp.bfloat16)
+    return fused(*args)
 
 
 def shards(queries, prefix_cache, *others):

time: 66.5 us -> 50.7 us (0.76)
  Pallas kernels: 62.4 us -> 48.7 us
  matrix products: 2.37 us -> 0 us
    pallas_call x1, Pallas kernels: 62.4 us -> 48.7 us  [fused(): pl.pallas_call(fused_kernel, in_specs=[smem, smem, vmem, hbm, hbm, hbm, h...]
    dot_general x1 -> x0, matrix products: 2.37 us -> none  [gather_plan(): lax.dot_general(placing, mixed, (((0,), (0,)), ((), ())), preferred_eleme...]
where the time goes in v2:
time: 50.7 us; the launch traced here: 50.6 us
  Pallas kernels  48.7 us (96%)
  local copies, waits for them, and re-layouts  1.87 us (4%)
    pallas_call x1, Pallas kernels, fused(): pl.pallas_call(fused_kernel, in_specs=[smem, smem, vmem, hbm, hbm, hbm, h...  48.7 us
    unnamed x1, local copies, waits for them, and re-layouts  1.87 us

profile of v2, /device:TPU:0, one launch (start us, length us, event | category | flops | bytes accessed | tf_op | source)
XLA Modules:
  0.0 50.6 jit_solution(10988349098508063386)
XLA Ops:
  0.0 48.7 %fused.1 = bf16[64,4096]{1,0:T(8,128)(2,1)} custom-call(s32[8]{0:T(128)} %slot_ref.1, s32[64]{0:T(128)} %lens_ref.1, s32[1,64]{1,0:T(1,128)} %bitcast.1, bf16[1,576,256]{2,1,0:T(8,128)(2,1)} %own.1, bf16[64,18432]{1,0:T(8,128)(2,1)} %q_hbm.1, bf16[64,576,128]{2,1,0:T(8,128)(2,1)} %suffix_hbm.1, bf16[32,512,128]{2,1,0:T(8,128)(2,1)} %w_hbm.1), custom_call_target="tpu_custom_call" | custom-call | tf_op jit(solution)/shard_map/fused/pallas_call | solution.py:735
  48.7 1.9 %copy.9 = bf16[64,4096]{1,0:T(8,128)(2,1)} copy(bf16[64,4096]{1,0:T(8,128)(2,1)} %fused.1) | data formatting | bytes 1048576
